TPU v7x, 1024 devices: a whole 8x8x8 slice. The times are simulated.
1024 devices in a mesh: gx: 128 (over y, z, core), gy: 8 (over x).
Axes of the slice: x: 8, y: 8, z: 8, core: 2. Of those that a mesh axis runs over, the one named last changes fastest.
Arguments:
- positions: float32 [3, 1024, 64, 128], P(None, 'gx', 'gy'), may hold values from 0 to 12
- charges: float32 [1024, 64, 128], P('gx', 'gy'), may hold values from -4 to 4
- cell_index: int32 [1024, 64, 128], P('gx', 'gy'), may hold values from 0 to 32767, as said below
- task_patch: int32 [128, 8, 32], P('gx', 'gy'), may hold values from 0 to 63
- task_near: int32 [128, 8, 32], P('gx', 'gy'), may hold values from 0 to 8
- task_count: int32 [128, 8], P('gx', 'gy'), may hold values from 1 to 32, as said below
Outputs:
- forces: float32 [3, 1024, 64, 128], P(None, 'gx', 'gy')
- recip_potential: float32 [1024, 64, 128], P('gx', 'gy')
Inputs may be any that keep to these rules, and one draw needn't show every extreme that they name: `task_near`: code k names the neighbouring patch at offset (k // 3 - 1, k % 3 - 1) along the two patch dimensions; only slots below task_count are read. `task_patch`: only slots below task_count are read. `task_count`: in each gx row one device has 32 live tasks, and the counts of the devices that share a gx index sum to at most 8 * 16. Each atom lies in the cell that cell_index names: for an atom of local patch row r and column s with coordinates (a, b, e), the cell has z = floor(e * 256 / 12), x = (r * 4 + floor(a * 4 / 12)) // 8, y = (s * 32 + floor(b * 32 / 12)) // 8, and c = (z * 4 + x) * 32 + y.
All inputs are finite; a program needn't handle non-finite values.
Results may differ from a plain program's by a relative error of at most 0.0003.
Values sent between devices are 32-bit elements; how exact they have to be, the bound alone decides.
A program may use at most 32 MiB of HBM per device.

v0:
```python
import math

import jax
import jax.numpy as jnp
from jax import lax
from jax.sharding import PartitionSpec as P

XR = 4
YC = 32
GZ = 256


SCREEN = 72.0
PATCH_SIDE = 12.0
KERNEL_SCALE = 64.0


def with_halo(value, sides, width):
    for axis, dim in sides:
        count, length = (lax.axis_size(axis), value.shape[dim])
        up = [(i, (i + 1) % count) for i in range(count)]
        down = [(j, i) for i, j in up]
        last = lax.slice_in_dim(value, length - width, length, axis=dim)
        initial = lax.slice_in_dim(value, 0, width, axis=dim)
        before = lax.ppermute(last, axis, up)
        after = lax.ppermute(initial, axis, down)
        value = jnp.concatenate([before, value, after], axis=dim)
    return value


def pair_force(first, second):
    delta = first[:3, :, None] - second[:3, None, :]
    dist_sq = jnp.sum(delta * delta, axis=0)
    strength = jnp.exp(-dist_sq / SCREEN) * (dist_sq + 1.0) ** (-1.5)
    weight = first[3][:, None] * second[3][None, :] * strength
    return jnp.sum(weight[None] * delta, axis=2)


def task_inputs(halo, patch, near):
    rows = halo.shape[1] - 2
    cols = halo.shape[2] - 2
    flat = halo.reshape(4, (rows + 2) * (cols + 2), halo.shape[3])
    prow = patch // cols + 1
    pcol = patch % cols + 1
    drow = near // 3 - 1
    dcol = near % 3 - 1
    first = jnp.take(flat, prow * (cols + 2) + pcol, axis=1)
    second = jnp.take(flat, (prow + drow) * (cols + 2) + pcol + dcol, axis=1)
    zeros = jnp.zeros(patch.shape, jnp.float32)
    shift = jnp.stack(
        [drow.astype(jnp.float32) * PATCH_SIDE, dcol.astype(jnp.float32) * PATCH_SIDE, zeros, zeros]
    )
    second = second + shift[:, :, None]
    return (jnp.moveaxis(first, 1, 0), jnp.moveaxis(second, 1, 0))


def patch_sum(per_task_force, patch, live, rows, cols):
    indicator_matrix = (
        (patch[:, None] == jnp.arange(rows * cols, dtype=jnp.int32)[None, :]) & live[:, None]
    ).astype(jnp.float32)
    accumulated_sum = jnp.einsum(
        "ew,esh->swh", indicator_matrix, per_task_force, precision=lax.Precision.HIGHEST
    )
    return accumulated_sum.reshape(3, rows, cols, per_task_force.shape[2])


def cas_table(length):
    steps = jnp.arange(length, dtype=jnp.int32)
    product = steps[:, None] * steps[None, :] % length
    angle = 2.0 * math.pi / length * product.astype(jnp.float32)
    return jnp.cos(angle) + jnp.sin(angle)


def wave_part(freq, length):
    folded = jnp.minimum(freq, length - freq).astype(jnp.float32) / length
    return folded * folded


def influence(depth_freq, row_freq, column_freq, depth_len, row_len, column_len):
    wave_sq = (
        wave_part(depth_freq, depth_len)[:, None, None]
        + wave_part(row_freq, row_len)[None, :, None]
        + wave_part(column_freq, column_len)[None, None, :]
    )
    safe = jnp.where(wave_sq > 0, wave_sq, 1.0)
    return jnp.where(wave_sq > 0, 1.0 / (KERNEL_SCALE * safe), 0.0)


def line_along_y(piece):
    return jnp.einsum(
        "zxy,yk->zxk", piece, cas_table(piece.shape[2]), precision=lax.Precision.HIGHEST
    )


def line_along_x(piece):
    return jnp.einsum(
        "zxy,xm->zmy", piece, cas_table(piece.shape[1]), precision=lax.Precision.HIGHEST
    )


def body(positions, charges, cell_index, task_patch, task_near, task_count):
    high = lax.Precision.HIGHEST
    rows = positions.shape[1]
    cols = positions.shape[2]
    atoms = jnp.concatenate([positions, charges[None]], axis=0)
    halo = with_halo(atoms, (("gx", 1), ("gy", 2)), 1)
    patch = task_patch.reshape(-1)
    near = task_near.reshape(-1)
    count = task_count.reshape(())
    slots = patch.shape[0]
    live = jnp.arange(slots, dtype=jnp.int32) < count
    first, second = task_inputs(halo, patch, near)
    per_task_force = jax.vmap(pair_force)(first, second)
    forces = patch_sum(per_task_force, patch, live, rows, cols)
    block_cells = XR * YC
    charge_flat = charges.reshape(-1)
    cells = cell_index.reshape(-1)
    onehot_depth = (
        (cells // block_cells)[:, None] == jnp.arange(GZ, dtype=jnp.int32)[None, :]
    ).astype(jnp.float32)
    onehot_flat = (
        (cells % block_cells)[:, None] == jnp.arange(block_cells, dtype=jnp.int32)[None, :]
    ).astype(jnp.float32)
    grid = jnp.dot(
        onehot_depth.T,
        charge_flat[:, None] * onehot_flat,
        precision=high,
        preferred_element_type=jnp.float32,
    )
    cas_z = cas_table(GZ)
    ztrans = jnp.dot(cas_z, grid, precision=high, preferred_element_type=jnp.float32).reshape(
        GZ, XR, YC
    )
    ytrans = line_along_y(lax.all_to_all(ztrans, "gy", split_axis=0, concat_axis=2, tiled=True))
    xtrans = line_along_x(lax.all_to_all(ytrans, "gx", split_axis=2, concat_axis=1, tiled=True))
    depth_share = xtrans.shape[0]
    total_x = xtrans.shape[1]
    width_share = xtrans.shape[2]
    total_y = width_share * lax.axis_size("gx")
    depth_freq = lax.axis_index("gy") * depth_share + jnp.arange(depth_share, dtype=jnp.int32)
    column_freq = lax.axis_index("gx") * width_share + jnp.arange(width_share, dtype=jnp.int32)
    kernel = influence(
        depth_freq, jnp.arange(total_x, dtype=jnp.int32), column_freq, GZ, total_x, total_y
    )
    scaled = xtrans * kernel
    xback = jnp.einsum("zmy,mx->zxy", scaled, cas_table(total_x), precision=high)
    rows_back = lax.all_to_all(xback, "gx", split_axis=1, concat_axis=2, tiled=True)
    yback = jnp.einsum("zxk,ky->zxy", rows_back, cas_table(total_y), precision=high)
    planes_back = lax.all_to_all(yback, "gy", split_axis=2, concat_axis=0, tiled=True)
    field = jnp.dot(
        cas_z,
        planes_back.reshape(GZ, block_cells),
        precision=high,
        preferred_element_type=jnp.float32,
    ) / (total_x * total_y * GZ)
    sampled = jnp.dot(onehot_depth, field, precision=high, preferred_element_type=jnp.float32)
    recip_potential = jnp.sum(onehot_flat * sampled, axis=1).reshape(charges.shape)
    return (forces, recip_potential)


def solution(mesh):
    return jax.shard_map(
        body,
        mesh=mesh,
        in_specs=(
            P(None, "gx", "gy", None),
            P("gx", "gy", None),
            P("gx", "gy", None),
            P("gx", "gy", None),
            P("gx", "gy", None),
            P("gx", "gy"),
        ),
        out_specs=(P(None, "gx", "gy", None), P("gx", "gy", None)),
        check_vma=False,
    )
```

profile of v0, /device:TPU:1, one launch (start us, length us, event | category | flops | bytes accessed | tf_op | source)
XLA Modules:
  0.0 139.7 jit_solution(18245052545157331178)
XLA Ops:
  1.4 6.3 %collective-permute-start = (f32[4,1,8,128]{3,2,1,0:T(8,128)S(1)}, f32[4,1,8,128]{3,2,1,0:T(8,128)S(1)}, u32[]{:S(2)}, u32[]{:S(2)}) collective-permute-start(f32[4,1,8,128]{3,2,1,0:T(8,128)S(1)} %get-tuple-element.11), channel_id=1, source_target_pairs={{0,8},{8,16},{16,24},{24,32},{32,40},{40,48},{48,56},{56,64},{64,7... | collective-permute-start | bytes 49160 | tf_op jit(solution)/shard_map/ppermute | solution.py:25
  7.7 11.7 %collective-permute-start.1 = (f32[4,1,8,128]{3,2,1,0:T(8,128)S(1)}, f32[4,1,8,128]{3,2,1,0:T(8,128)S(1)}, u32[]{:S(2)}, u32[]{:S(2)}) collective-permute-start(f32[4,1,8,128]{3,2,1,0:T(8,128)S(1)} %get-tuple-element.12), channel_id=1, source_target_pairs={{8,0},{16,8},{24,16},{32,24},{40,32},{48,40},{56,48},{64,56},{72,6... | collective-permute-start | bytes 49160 | tf_op jit(solution)/shard_map/ppermute | solution.py:26
  20.1 6.6 %fusion.3 = f32[256,128]{1,0:T(8,128)S(1)} fusion(s32[8192]{0:T(1024)S(1)} %get-tuple-element.14, f32[8192]{0:T(1024)} %bitcast.174, s32[8192]{0:T(1024)S(1)} %get-tuple-element.13), kind=kOutput, calls=%fused_computation.9 | convolution fusion | flops 3227516928 | bytes 229376 | tf_op jit(solution)/shard_map/dot_general | solution.py:124
  26.8 1.5 %fusion.34 = f32[256,128]{0,1:T(8,128)S(1)} fusion(f32[256,128]{1,0:T(8,128)S(1)} %fusion.3), kind=kOutput, calls=%fused_computation.58 | convolution fusion | flops 101646336 | bytes 262144 | tf_op jit(solution)/shard_map/dot_general | solution.py:131
  28.5 1.0 reshape.287
  29.5 3.4 %all-to-all-start = ((f32[8,1,4096]{2,1,0:T(1,128)}), f32[8,1,4096]{2,1,0:T(1,128)S(1)}, u32[]{:S(2)}, u32[]{:S(2)}) async-start(f32[8,1,4096]{2,1,0:T(1,128)} %reshape.287), calls=%async_computation | async-start | bytes 262144 | tf_op jit(solution)/shard_map/all_to_all | solution.py:134
  34.0 3.3 %collective-permute-start.2 = (f32[4,10,1,128]{3,2,1,0:T(1,128)S(1)}, f32[4,10,1,128]{3,2,1,0:T(1,128)S(1)}, u32[]{:S(2)}, u32[]{:S(2)}) collective-permute-start(f32[4,10,1,128]{3,2,1,0:T(1,128)S(1)} %get-tuple-element.9), channel_id=1, source_target_pairs={{0,1},{1,2},{2,3},{3,4},{4,5},{5,6},{6,7},{7,0},{8,9},{9,10},{10,1... | collective-permute-start | bytes 61448 | tf_op jit(solution)/shard_map/ppermute | solution.py:25
  37.2 3.2 %collective-permute-start.3 = (f32[4,10,1,128]{3,2,1,0:T(1,128)S(1)}, f32[4,10,1,128]{3,2,1,0:T(1,128)S(1)}, u32[]{:S(2)}, u32[]{:S(2)}) collective-permute-start(f32[4,10,1,128]{3,2,1,0:T(1,128)S(1)} %get-tuple-element.10), channel_id=1, source_target_pairs={{1,0},{2,1},{3,2},{4,3},{5,4},{6,5},{7,6},{0,7},{9,8},{10,9},{11,1... | collective-permute-start | bytes 61448 | tf_op jit(solution)/shard_map/ppermute | solution.py:26
  40.6 1.2 collective-permute-done.3
  43.8 1.0 reduce
  45.6 1.3 fusion.26
  47.2 1.0 reshape.289
  48.1 18.2 %all-to-all-start.1 = ((f32[128,1,256]{2,1,0:T(1,128)}), f32[128,1,256]{2,1,0:T(1,128)S(1)}, u32[]{:S(2)}, u32[]{:S(2)}) async-start(f32[128,1,256]{2,1,0:T(1,128)} %reshape.289), calls=%async_computation.1 | async-start | bytes 262144 | tf_op jit(solution)/shard_map/all_to_all | solution.py:135
  66.5 2.1 %fusion.1 = f32[32,128,128]{2,1,0:T(8,128)S(1)} fusion(f32[32,3,128]{2,1,0:T(4,128)S(1)} %bitcast.165, f32[32,3,128]{2,1,0:T(4,128)S(1)} %bitcast.167), kind=kLoop, calls=%fused_computation.7 | loop fusion | flops 4194304 | bytes 2195456 | tf_op jit(solution)/shard_map/vmap()/reduce_sum | solution.py:33
  68.6 10.0 %all-to-all-done.1 = f32[128,1,256]{2,1,0:T(1,128)S(1)} async-done(((f32[128,1,256]{2,1,0:T(1,128)}), f32[128,1,256]{2,1,0:T(1,128)S(1)}, u32[]{:S(2)}, u32[]{:S(2)}) %all-to-all-start.1) | async-done | bytes 131104 | tf_op jit(solution)/shard_map/all_to_all | solution.py:135
  78.6 1.0 reduce.1
  80.2 5.7 %fusion.12 = f32[32,512,2]{1,0,2:T(8,128)S(1)} fusion(f32[32,512,2]{0,1,2:T(8,128)S(1)} %bitcast.171, f32[2]{0:T(128)S(1)} %fusion.55, f32[32,512]{1,0:T(8,128)S(1)} %broadcast_add_fusion), kind=kOutput, calls=%fused_computation.25 | convolution fusion | flops 205488128 | bytes 327688 | tf_op jit(solution)/shard_map/zxy,xm->zmy/dot_general | solution.py:96
  86.0 5.1 %convolution_bitcast_fusion = f32[32,512,2]{1,0,2:T(8,128)S(1)} fusion(f32[32,512,2]{1,0,2:T(8,128)S(1)} %fusion.12), kind=kOutput, calls=%fused_computation.23 | convolution fusion | flops 205258752 | bytes 262144 | tf_op jit(solution)/shard_map/zmy,mx->zxy/dot_general | solution.py:146
  91.4 1.2 reshape.291
  92.6 6.1 %all-to-all-start.2 = ((f32[128,1,256]{2,1,0:T(1,128)}), f32[128,1,256]{2,1,0:T(1,128)S(1)}, u32[]{:S(2)}, u32[]{:S(2)}) async-start(f32[128,1,256]{2,1,0:T(1,128)} %reshape.291), calls=%async_computation.2 | async-start | bytes 262144 | tf_op jit(solution)/shard_map/all_to_all | solution.py:147
  98.7 2.3 %multiply_multiply_fusion = f32[32,128,128]{2,1,0:T(8,128)} fusion(f32[32,128,128]{2,1,0:T(8,128)S(1)} %fusion.1, f32[32,128]{1,0:T(8,128)S(1)} %bitcast.178, f32[32,128]{1,0:T(8,128)S(1)} %bitcast.179), kind=kLoop, calls=%fused_computation.17 | loop fusion | flops 3145728 | bytes 4227072 | tf_op jit(solution)/shard_map/vmap()/mul | solution.py:35
  100.9 10.1 %all-to-all-done.2 = f32[128,1,256]{2,1,0:T(1,128)S(1)} async-done(((f32[128,1,256]{2,1,0:T(1,128)}), f32[128,1,256]{2,1,0:T(1,128)S(1)}, u32[]{:S(2)}, u32[]{:S(2)}) %all-to-all-start.2) | async-done | bytes 131104 | tf_op jit(solution)/shard_map/all_to_all | solution.py:147
  111.0 1.0 reduce.2
  112.9 1.7 %fusion.24 = f32[32,4,256]{2,0,1:T(8,128)S(1)} fusion(f32[32,4,256]{0,2,1:T(8,128)S(1)} %bitcast.172), kind=kOutput, calls=%fused_computation.45 | convolution fusion | flops 101646336 | bytes 262144 | tf_op jit(solution)/shard_map/zxk,ky->zxy/dot_general | solution.py:148
  114.9 1.0 reshape.293
  115.9 6.7 %all-to-all-start.3 = ((f32[8,1,4096]{2,1,0:T(1,128)}), f32[8,1,4096]{2,1,0:T(1,128)S(1)}, u32[]{:S(2)}, u32[]{:S(2)}) async-start(f32[8,1,4096]{2,1,0:T(1,128)} %reshape.293), calls=%async_computation.3 | async-start | bytes 262144 | tf_op jit(solution)/shard_map/all_to_all | solution.py:149
  122.6 3.7 %fusion.2 = f32[32,3,128]{2,1,0:T(4,128)S(1)} fusion(f32[32,128,128]{2,1,0:T(8,128)S(1)} %copy-done, f32[32,3,128]{2,1,0:T(4,128)S(1)} %bitcast.166, f32[32,3,128]{2,1,0:T(4,128)S(1)} %bitcast.168), kind=kLoop, calls=%fused_computation.8 | loop fusion | flops 4706304 | bytes 2244608 | tf_op jit(solution)/shard_map/vmap()/reduce_sum | solution.py:36
  126.3 1.0 convolution_bitcast_fusion.2
  127.2 3.3 %all-to-all-done.3 = f32[8,1,4096]{2,1,0:T(1,128)S(1)} async-done(((f32[8,1,4096]{2,1,0:T(1,128)}), f32[8,1,4096]{2,1,0:T(1,128)S(1)}, u32[]{:S(2)}, u32[]{:S(2)}) %all-to-all-start.3) | async-done | bytes 131104 | tf_op jit(solution)/shard_map/all_to_all | solution.py:149
  130.5 1.0 reduce.3
  132.2 1.6 %convolution_multiply_fusion = f32[256,128]{1,0:T(8,128)S(1)} fusion(f32[256,128]{0,1:T(8,128)S(1)} %reshape.260), kind=kOutput, calls=%fused_computation.22 | convolution fusion | flops 101679104 | bytes 262144 | tf_op jit(solution)/shard_map/dot_general | solution.py:150
  133.9 5.8 %fusion.11 = f32[8192]{0:T(1024)} fusion(f32[256,128]{1,0:T(8,128)S(1)} %convolution_multiply_fusion, s32[8192]{0:T(1024)S(1)} %get-tuple-element.14, s32[8192]{0:T(1024)S(1)} %get-tuple-element.13), kind=kOutput, calls=%fused_computation.18 | convolution fusion | flops 3226460160 | bytes 229376 | tf_op jit(solution)/shard_map/dot_general | solution.py:156
  (56 shorter events, 8.2 us)
Async XLA Ops:
  1.4 32.5 %collective-permute-start = (f32[4,1,8,128]{3,2,1,0:T(8,128)S(1)}, f32[4,1,8,128]{3,2,1,0:T(8,128)S(1)}, u32[]{:S(2)}, u32[]{:S(2)}) collective-permute-start(f32[4,1,8,128]{3,2,1,0:T(8,128)S(1)} %get-tuple-element.11), channel_id=1, source_target_pairs={{0,8},{8,16},{16,24},{24,32},{32,40},{40,48},{48,56},{56,64},{64,7... | collective-permute-start | bytes 49160 | tf_op jit(solution)/shard_map/ppermute | solution.py:25
  7.7 26.2 %collective-permute-start.1 = (f32[4,1,8,128]{3,2,1,0:T(8,128)S(1)}, f32[4,1,8,128]{3,2,1,0:T(8,128)S(1)}, u32[]{:S(2)}, u32[]{:S(2)}) collective-permute-start(f32[4,1,8,128]{3,2,1,0:T(8,128)S(1)} %get-tuple-element.12), channel_id=1, source_target_pairs={{8,0},{16,8},{24,16},{32,24},{40,32},{48,40},{56,48},{64,56},{72,6... | collective-permute-start | bytes 49160 | tf_op jit(solution)/shard_map/ppermute | solution.py:26
  26.7 6.1 %copy-start.4 = (s32[1,1,32]{2,1,0:T(1,128)S(1)}, s32[1,1,32]{2,1,0:T(1,128)}, u32[]{:S(2)}) copy-start(s32[1,1,32]{2,1,0:T(1,128)} %param.11) | copy-start | bytes 388
  26.8 6.2 %copy-start.3 = (s32[1,1,32]{2,1,0:T(1,128)S(1)}, s32[1,1,32]{2,1,0:T(1,128)}, u32[]{:S(2)}) copy-start(s32[1,1,32]{2,1,0:T(1,128)} %param.12) | copy-start | bytes 388
  26.8 7.1 %copy-start.1 = (f32[3,8,8,128]{3,2,1,0:T(8,128)S(1)}, f32[3,8,8,128]{3,2,1,0:T(8,128)}, u32[]{:S(2)}) copy-start(f32[3,8,8,128]{3,2,1,0:T(8,128)} %param.8) | copy-start | bytes 294916
  26.8 7.1 %copy-start.2 = (f32[8,8,128]{2,1,0:T(8,128)S(1)}, f32[8,8,128]{2,1,0:T(8,128)}, u32[]{:S(2)}) copy-start(f32[8,8,128]{2,1,0:T(8,128)} %param.9) | copy-start | bytes 98308
  29.5 13.8 %all-to-all-start = ((f32[8,1,4096]{2,1,0:T(1,128)}), f32[8,1,4096]{2,1,0:T(1,128)S(1)}, u32[]{:S(2)}, u32[]{:S(2)}) async-start(f32[8,1,4096]{2,1,0:T(1,128)} %reshape.287), calls=%async_computation | async-start | bytes 262144 | tf_op jit(solution)/shard_map/all_to_all | solution.py:134
  34.0 6.6 %collective-permute-start.2 = (f32[4,10,1,128]{3,2,1,0:T(1,128)S(1)}, f32[4,10,1,128]{3,2,1,0:T(1,128)S(1)}, u32[]{:S(2)}, u32[]{:S(2)}) collective-permute-start(f32[4,10,1,128]{3,2,1,0:T(1,128)S(1)} %get-tuple-element.9), channel_id=1, source_target_pairs={{0,1},{1,2},{2,3},{3,4},{4,5},{5,6},{6,7},{7,0},{8,9},{9,10},{10,1... | collective-permute-start | bytes 61448 | tf_op jit(solution)/shard_map/ppermute | solution.py:25
  37.2 4.5 %collective-permute-start.3 = (f32[4,10,1,128]{3,2,1,0:T(1,128)S(1)}, f32[4,10,1,128]{3,2,1,0:T(1,128)S(1)}, u32[]{:S(2)}, u32[]{:S(2)}) collective-permute-start(f32[4,10,1,128]{3,2,1,0:T(1,128)S(1)} %get-tuple-element.10), channel_id=1, source_target_pairs={{1,0},{2,1},{3,2},{4,3},{5,4},{6,5},{7,6},{0,7},{9,8},{10,9},{11,1... | collective-permute-start | bytes 61448 | tf_op jit(solution)/shard_map/ppermute | solution.py:26
  48.1 30.5 %all-to-all-start.1 = ((f32[128,1,256]{2,1,0:T(1,128)}), f32[128,1,256]{2,1,0:T(1,128)S(1)}, u32[]{:S(2)}, u32[]{:S(2)}) async-start(f32[128,1,256]{2,1,0:T(1,128)} %reshape.289), calls=%async_computation.1 | async-start | bytes 262144 | tf_op jit(solution)/shard_map/all_to_all | solution.py:135
  92.6 18.5 %all-to-all-start.2 = ((f32[128,1,256]{2,1,0:T(1,128)}), f32[128,1,256]{2,1,0:T(1,128)S(1)}, u32[]{:S(2)}, u32[]{:S(2)}) async-start(f32[128,1,256]{2,1,0:T(1,128)} %reshape.291), calls=%async_computation.2 | async-start | bytes 262144 | tf_op jit(solution)/shard_map/all_to_all | solution.py:147
  112.5 10.1 %copy-start = (f32[32,128,128]{2,1,0:T(8,128)S(1)}, f32[32,128,128]{2,1,0:T(8,128)}, u32[]{:S(2)}) copy-start(f32[32,128,128]{2,1,0:T(8,128)} %multiply_multiply_fusion) | copy-start | bytes 6291460
  115.9 14.6 %all-to-all-start.3 = ((f32[8,1,4096]{2,1,0:T(1,128)}), f32[8,1,4096]{2,1,0:T(1,128)S(1)}, u32[]{:S(2)}, u32[]{:S(2)}) async-start(f32[8,1,4096]{2,1,0:T(1,128)} %reshape.293), calls=%async_computation.3 | async-start | bytes 262144 | tf_op jit(solution)/shard_map/all_to_all | solution.py:149
where the time goes:
time: 140 us
  starting transfers between devices  58.8 us (42%)
  matrix products  30.4 us (22%)
  waiting for transfers between devices  24.6 us (18%)
  other arithmetic  13.9 us (10%)
  local copies, waits for them, and re-layouts  10.2 us (7%)
  between operations  1.74 us (1%)
    all_to_all x1, starting transfers between devices, body(): lax.all_to_all(ytrans, 'gx', split_axis=2, concat_axis=1, tiled=True)  18.2 us
    ppermute x2, starting transfers between devices, with_halo(): after = lax.ppermute(initial, axis, down)  14.9 us
    all_to_all x1, waiting for transfers between devices, body(): lax.all_to_all(xback, 'gx', split_axis=1, concat_axis=2, tiled=True)  10.1 us
    all_to_all x1, waiting for transfers between devices, body(): lax.all_to_all(ytrans, 'gx', split_axis=2, concat_axis=1, tiled=True)  10 us
    ppermute x2, starting transfers between devices, with_halo(): before = lax.ppermute(last, axis, up)  9.54 us
    all_to_all x1, starting transfers between devices, body(): lax.all_to_all(yback, 'gy', split_axis=2, concat_axis=0, tiled=True)  6.68 us
    dot_general x1, matrix products, body(): jnp.dot(onehot_depth.T, charge_flat[:, None] * onehot_flat, precision=hig...  6.61 us
    all_to_all x1, starting transfers between devices, body(): lax.all_to_all(xback, 'gx', split_axis=1, concat_axis=2, tiled=True)  6.07 us
  transfers between devices with their start and end apart: 8, of which 4 were waited for; matrix products, arithmetic and copies ran while one was open for 15% of the time, Pallas kernels for 0%

commit v1 on v0

v1 whole, which is shorter than its diff:
```python
import functools

import jax
import jax.numpy as jnp
import numpy as np
from jax import lax
from jax.experimental import pallas as pl
from jax.experimental.pallas import tpu as pltpu
from jax.sharding import PartitionSpec as P

MESH_ID = pl.DeviceIdType.MESH
F32 = jnp.float32
BF16 = jnp.bfloat16

NX = 128
NY = 8
GX = 512
GY = 256
GZ = 256
TASKS = 32
PATCH_SIDE = 12.0
EXP_SCALE = -1.0 / 72.0


def cas_split(length, rows=None):
    steps = np.arange(length, dtype=np.int64)
    angle = (2.0 * np.pi / length) * ((steps[:, None] * steps[None, :]) % length)
    table = np.cos(angle) + np.sin(angle)
    if rows is not None:
        table = table[:, rows]
    high = table.astype(np.float32).astype(BF16)
    low = (table - high.astype(np.float64)).astype(np.float32).astype(BF16)
    return np.stack([high, low])


def split(value):
    high = value.astype(BF16)
    low = (value - high.astype(F32)).astype(BF16)
    return high, low


def mxu(a, b, dims=((1,), (0,))):
    return lax.dot_general(a, b, (dims, ((), ())), preferred_element_type=F32)


def left_table(table, value):
    high, low = split(value)
    both = mxu(table[0], jnp.concatenate([high, low], axis=1))
    return both[:, :128] + both[:, 128:] + mxu(table[1], high)


def right_table(value, table):
    high, low = split(value)
    m = value.shape[0]
    both = mxu(jnp.concatenate([high, low], axis=0), table[0])
    return both[:m] + both[m:] + mxu(high, table[1])


def lane_block(shape):
    return lax.broadcasted_iota(jnp.int32, shape, 1) // 32


def pick(blocks, lanes):
    out = blocks[3]
    for b in (2, 1, 0):
        out = jnp.where(lanes == b, blocks[b], out)
    return out


def turn(value, blocks):
    blocks = blocks % 4
    return value if blocks == 0 else pltpu.roll(value, 32 * blocks, 1)


def kernel(
    patch_s,
    near_s,
    count_s,
    patch_ref,
    pos_hbm,
    chg_hbm,
    cell_hbm,
    casz_hbm,
    casy_hbm,
    casx_hbm,
    casxt_hbm,
    forces_hbm,
    recip_hbm,
    pos_ref,
    chg_ref,
    cell_ref,
    forces_ref,
    recip_ref,
    casz,
    casy,
    casx,
    casxt,
    halo,
    onehot,
    grid_t,
    influence,
    second,
    task_force,
    send_a,
    recv_a,
    send_b,
    recv_b,
    send_c,
    recv_c,
    send_d,
    recv_d,
    load_sem,
    store_sem,
    halo_send,
    halo_recv,
    ex_send,
    ex_recv,
):
    gx = lax.axis_index("gx")
    gy = lax.axis_index("gy")
    up = lax.rem(gx + 1, NX)
    down = lax.rem(gx + NX - 1, NX)
    right = lax.rem(gy + 1, NY)
    left = lax.rem(gy + NY - 1, NY)
    chip_y, chip_z, core = gx // 16, (gx // 2) % 8, gx % 2

    def column_peer(k):
        dc, dz, dy = k % 2, (k // 2) % 8, k // 16
        return (
            lax.rem(chip_y + dy, 8) * 16 + lax.rem(chip_z + dz, 8) * 2 + lax.rem(core + dc, 2)
        )

    loads = [
        pltpu.make_async_copy(src, dst, load_sem.at[i])
        for i, (src, dst) in enumerate(
            (
                (cell_hbm, cell_ref),
                (chg_hbm, chg_ref),
                (pos_hbm, pos_ref),
                (casz_hbm, casz),
                (casy_hbm, casy),
                (casx_hbm, casx),
                (casxt_hbm, casxt),
            )
        )
    ]
    for load in loads:
        load.start()
    tables = loads[3:]

    barrier = pltpu.get_barrier_semaphore()
    for d in range(1, NY):
        pl.semaphore_signal(
            barrier, 1, device_id={"gx": gx, "gy": lax.rem(gy + d, NY)}, device_id_type=MESH_ID
        )
    for px in (up, down):
        for py in (left, right):
            pl.semaphore_signal(barrier, 1, device_id={"gx": px, "gy": py}, device_id_type=MESH_ID)

    def greet(k, carry):
        pl.semaphore_signal(
            barrier, 1, device_id={"gx": column_peer(k), "gy": gy}, device_id_type=MESH_ID
        )
        return carry

    lax.fori_loop(1, NX, greet, 0)

    for load in loads[:3]:
        load.wait()

    for r in range(8):
        for c in range(3):
            halo[r + 1, 1:9, c, :] = pos_ref[c, r]
        halo[r + 1, 1:9, 3, :] = chg_ref[r]

    z_row = lax.broadcasted_iota(jnp.int32, (GZ, 256), 0)
    eight = lax.broadcasted_iota(jnp.int32, (8, 256), 0)

    def deposit(x, carry):
        for s in range(8):
            cells = jnp.concatenate(
                [cell_ref[2 * x, s : s + 1, :], cell_ref[2 * x + 1, s : s + 1, :]], axis=1
            )
            charge = jnp.concatenate(
                [chg_ref[2 * x, s : s + 1, :], chg_ref[2 * x + 1, s : s + 1, :]], axis=1
            )
            hot = jnp.where(z_row == cells // 128, 1.0, 0.0).astype(BF16)
            onehot[x * 8 + s] = hot
            high = charge.astype(BF16).astype(F32)
            rows = jnp.where(eight < 4, high, charge - high)
            rows = jnp.where(eight % 4 == cells % 4, rows, 0.0).astype(BF16)
            part = mxu(rows, hot, ((1,), (1,)))
            grid_t[x, s] = part[0:4] + part[4:8]
        return carry

    lax.fori_loop(0, 4, deposit, 0)

    kx = lax.broadcasted_iota(jnp.int32, (GX, 128), 0)
    lane = lax.broadcasted_iota(jnp.int32, (GX, 128), 1)
    kz = gy * 32 + lane % 32
    ky = gx * 2 + (lane // 32) % 2

    def wave(freq, length):
        part = jnp.minimum(freq, length - freq).astype(F32) * (1.0 / length)
        return part * part

    wave_sq = wave(kz, GZ) + wave(kx, GX) + wave(ky, GY)
    influence[...] = jnp.where(
        wave_sq > 0, 1.0 / (64.0 * jnp.where(wave_sq > 0, wave_sq, 1.0)), 0.0
    )

    tables[0].wait()
    ztrans = right_table(grid_t[...].reshape(128, GZ), casz)
    quarter = lane_block((32, 128))
    for h in range(2):
        parts = [ztrans[32 * x : 32 * x + 32, 128 * h : 128 * h + 128] for x in range(4)]
        for m in range(4):
            send_a[4 * h + m] = pick([turn(parts[x], x - m) for x in range(4)], quarter)

    pl.semaphore_wait(barrier, NY - 1 + 4 + NX - 1)

    def row_exchange(src, dst, which):
        for d in (4, 3, 5, 2, 6, 1, 7):
            peer = lax.rem(gy + d, NY)
            pltpu.make_async_remote_copy(
                src.at[peer],
                dst.at[gy],
                ex_send.at[which],
                ex_recv.at[which],
                device_id={"gx": gx, "gy": peer},
                device_id_type=MESH_ID,
            ).start()
        dst[gy] = src[gy]

    def row_wait(src, dst, which):
        pltpu.make_async_remote_copy(
            src.at[pl.ds(0, NY - 1)],
            dst.at[pl.ds(0, NY - 1)],
            ex_send.at[which],
            ex_recv.at[which],
            device_id={"gx": gx, "gy": right},
            device_id_type=MESH_ID,
        ).wait()

    def column_exchange(src, dst, which):
        def send(i, carry):
            peer = column_peer(NX - 1 - i)
            pltpu.make_async_remote_copy(
                src.at[peer],
                dst.at[gx],
                ex_send.at[which],
                ex_recv.at[which],
                device_id={"gx": peer, "gy": gy},
                device_id_type=MESH_ID,
            ).start()
            return carry

        lax.fori_loop(0, NX - 1, send, 0)
        dst[gx] = src[gx]

    def column_wait(src, dst, which):
        pltpu.make_async_remote_copy(
            src.at[pl.ds(0, NX - 1)],
            dst.at[pl.ds(0, NX - 1)],
            ex_send.at[which],
            ex_recv.at[which],
            device_id={"gx": up, "gy": gy},
            device_id_type=MESH_ID,
        ).wait()

    row_exchange(send_a, recv_a, 0)

    halo_copies = []
    for n, (dx, dy) in enumerate(
        ((-1, -1), (-1, 0), (-1, 1), (0, -1), (0, 1), (1, -1), (1, 0), (1, 1))
    ):
        px = (down, gx, up)[dx + 1]
        py = (left, gy, right)[dy + 1]
        src_r = {-1: pl.ds(1, 1), 0: pl.ds(1, 8), 1: pl.ds(8, 1)}[dx]
        dst_r = {-1: pl.ds(9, 1), 0: pl.ds(1, 8), 1: pl.ds(0, 1)}[dx]
        src_c = {-1: pl.ds(1, 1), 0: pl.ds(1, 8), 1: pl.ds(8, 1)}[dy]
        dst_c = {-1: pl.ds(9, 1), 0: pl.ds(1, 8), 1: pl.ds(0, 1)}[dy]
        copy = pltpu.make_async_remote_copy(
            halo.at[src_r, src_c],
            halo.at[dst_r, dst_c],
            halo_send.at[n],
            halo_recv.at[n],
            device_id={"gx": px, "gy": py},
            device_id_type=MESH_ID,
        )
        copy.start()
        halo_copies.append(copy)

    tables[1].wait()
    row_wait(send_a, recv_a, 0)
    ytrans = left_table(casy, recv_a[...].reshape(GY, 128))
    send_b[...] = ytrans.reshape(NX, 2, 128)
    column_exchange(send_b, recv_b, 1)

    for copy in halo_copies:
        copy.wait()

    def task_group(g, carry):
        firsts = []
        for t in range(8):
            patch = patch_s[0, 0, 8 * g + t]
            near = near_s[0, 0, 8 * g + t]
            prow, pcol = patch // 8 + 1, patch % 8 + 1
            drow, dcol = near // 3 - 1, near % 3 - 1
            firsts.append((prow, pcol, drow, dcol))
            second[4 * t : 4 * t + 4, :] = halo[prow + drow, pcol + dcol]
        columns = jnp.transpose(second[...])
        for t in range(8):
            prow, pcol, drow, dcol = firsts[t]
            first = halo[prow, pcol]
            ax = first[0:1] - drow.astype(F32) * PATCH_SIDE
            ay = first[1:2] - dcol.astype(F32) * PATCH_SIDE
            az = first[2:3]
            sums = [jnp.zeros((8, 128), F32) for _ in range(3)]
            for chunk in range(4):
                b = columns[32 * chunk : 32 * chunk + 32]
                delta = [
                    a - b[:, 4 * t + c : 4 * t + c + 1] for c, a in enumerate((ax, ay, az))
                ]
                dist = delta[0] * delta[0] + delta[1] * delta[1] + delta[2] * delta[2]
                inv = lax.rsqrt(dist + 1.0)
                weight = b[:, 4 * t + 3 : 4 * t + 4] * jnp.exp(dist * EXP_SCALE) * (inv * inv * inv)
                for c in range(3):
                    term = weight * delta[c]
                    sums[c] = sums[c] + (
                        (term[0:8] + term[8:16]) + (term[16:24] + term[24:32])
                    )
            for c in range(3):
                total = jnp.sum(sums[c], axis=0, keepdims=True) * first[3:4]
                task_force[c, pl.ds(8 * g + t, 1), :] = total
        return carry

    lax.fori_loop(0, TASKS // 8, task_group, 0)
    slot = lax.broadcasted_iota(jnp.int32, (64, TASKS), 1)
    owner = lax.broadcasted_iota(jnp.int32, (64, TASKS), 0)
    acts = jnp.where((owner == patch_ref[0]) & (slot < count_s[0, 0]), 1.0, 0.0).astype(BF16)
    for c in range(3):
        force = task_force[c]
        high = force.astype(BF16)
        rest = force - high.astype(F32)
        mid = rest.astype(BF16)
        low = (rest - mid.astype(F32)).astype(BF16)
        total = mxu(acts, high) + (mxu(acts, mid) + mxu(acts, low))
        forces_ref[c] = total.reshape(8, 8, 128)
    forces_out = pltpu.make_async_copy(forces_ref, forces_hbm, store_sem.at[0])
    forces_out.start()

    tables[2].wait()
    tables[3].wait()
    column_wait(send_b, recv_b, 1)
    lanes = lane_block((NX, 128))
    low_half = lax.broadcasted_iota(jnp.int32, (NX, 128), 1) < 64
    lines = [recv_b[:, e, :] for e in range(2)]
    turned = [[turn(lines[e], d) for d in range(4)] for e in range(2)]
    packed = []
    for x in range(4):
        value = pick([turned[b % 2][(b - x) % 4] for b in range(4)], lanes)
        high = value.astype(BF16).astype(F32)
        packed.append(jnp.where(low_half, high, value - high).astype(BF16))
    packed = jnp.concatenate(packed, axis=0)
    total = mxu(casx[0], packed) + mxu(casx[1], packed)
    scaled = (total + pltpu.roll(total, 64, 1)) * influence[...]
    high = scaled.astype(BF16).astype(F32)
    half = lax.broadcasted_iota(jnp.int32, (GX, 128), 1) < 64
    packed = jnp.where(half, high, scaled - high).astype(BF16)
    total = mxu(casxt[0], packed) + mxu(casxt[1], packed)
    xback = total + pltpu.roll(total, 64, 1)
    plain = [xback[128 * x : 128 * x + 128] for x in range(4)]
    moved = [turn(p, 1) for p in plain]
    send_c[:, 0, :] = pick([plain[0], moved[1], plain[2], moved[3]], lanes)
    send_c[:, 1, :] = pick([moved[0], plain[1], moved[2], plain[3]], lanes)
    column_exchange(send_c, recv_c, 2)

    column_wait(send_c, recv_c, 2)
    yback = left_table(casy, recv_c[...].reshape(GY, 128))
    send_d[...] = yback.reshape(NY, 32, 128)
    row_exchange(send_d, recv_d, 3)
    row_wait(send_d, recv_d, 3)

    rows = []
    for x in range(4):
        halves = []
        for h in range(2):
            halves.append(
                pick([turn(recv_d[4 * h + m], m - x) for m in range(4)], quarter)
            )
        rows.append(jnp.concatenate(halves, axis=1))
    field = right_table(jnp.concatenate(rows, axis=0), casz) * (1.0 / (GX * GY * GZ))
    grid_t[...] = field.reshape(4, 8, 4, GZ)

    def sample(x, carry):
        for s in range(8):
            cells = jnp.concatenate(
                [cell_ref[2 * x, s : s + 1, :], cell_ref[2 * x + 1, s : s + 1, :]], axis=1
            )
            value = grid_t[x, s]
            high = value.astype(BF16).astype(F32)
            both = jnp.concatenate([high, value - high], axis=0).astype(BF16)
            got = mxu(both, onehot[x * 8 + s])
            got = jnp.sum(jnp.where(eight % 4 == cells % 4, got, 0.0), axis=0, keepdims=True)
            recip_ref[2 * x, s : s + 1, :] = got[:, :128]
            recip_ref[2 * x + 1, s : s + 1, :] = got[:, 128:]
        return carry

    lax.fori_loop(0, 4, sample, 0)
    recip_out = pltpu.make_async_copy(recip_ref, recip_hbm, store_sem.at[1])
    recip_out.start()
    forces_out.wait()
    recip_out.wait()


def body(positions, charges, cell_index, task_patch, task_near, task_count):
    casz = cas_split(GZ)
    casy = cas_split(GY)
    order = (4 * np.arange(NX)[None, :] + np.arange(4)[:, None]).reshape(-1)
    casx = cas_split(GX, order)
    casxt = np.ascontiguousarray(np.swapaxes(casx, 1, 2))
    vmem = pl.BlockSpec(memory_space=pltpu.VMEM)
    smem = pl.BlockSpec(memory_space=pltpu.SMEM)
    hbm = pl.BlockSpec(memory_space=pltpu.HBM)
    return pl.pallas_call(
        kernel,
        out_shape=(
            jax.ShapeDtypeStruct((3, 8, 8, 128), F32),
            jax.ShapeDtypeStruct((8, 8, 128), F32),
        ),
        in_specs=[smem] * 3 + [vmem] + [hbm] * 7,
        out_specs=(hbm, hbm),
        scratch_shapes=[
            pltpu.VMEM((3, 8, 8, 128), F32),
            pltpu.VMEM((8, 8, 128), F32),
            pltpu.VMEM((8, 8, 128), jnp.int32),
            pltpu.VMEM((3, 8, 8, 128), F32),
            pltpu.VMEM((8, 8, 128), F32),
            pltpu.VMEM((2, GZ, GZ), BF16),
            pltpu.VMEM((2, GY, GY), BF16),
            pltpu.VMEM((2, GX, GX), BF16),
            pltpu.VMEM((2, GX, GX), BF16),
            pltpu.VMEM((10, 10, 4, 128), F32),
            pltpu.VMEM((32, GZ, 256), BF16),
            pltpu.VMEM((4, 8, 4, GZ), F32),
            pltpu.VMEM((GX, 128), F32),
            pltpu.VMEM((32, 128), F32),
            pltpu.VMEM((3, TASKS, 128), F32),
            pltpu.VMEM((NY, 32, 128), F32),
            pltpu.VMEM((NY, 32, 128), F32),
            pltpu.VMEM((NX, 2, 128), F32),
            pltpu.VMEM((NX, 2, 128), F32),
            pltpu.VMEM((NX, 2, 128), F32),
            pltpu.VMEM((NX, 2, 128), F32),
            pltpu.VMEM((NY, 32, 128), F32),
            pltpu.VMEM((NY, 32, 128), F32),
            pltpu.SemaphoreType.DMA((7,)),
            pltpu.SemaphoreType.DMA((2,)),
            pltpu.SemaphoreType.DMA((8,)),
            pltpu.SemaphoreType.DMA((8,)),
            pltpu.SemaphoreType.DMA((4,)),
            pltpu.SemaphoreType.DMA((4,)),
        ],
        compiler_params=pltpu.CompilerParams(
            collective_id=0, has_side_effects=True, vmem_limit_bytes=67_043_328
        ),
        name="patch_forces_and_grid",
    )(
        task_patch,
        task_near,
        task_count,
        task_patch,
        positions,
        charges,
        cell_index,
        casz,
        casy,
        casx,
        casxt,
    )


def solution(mesh):
    return jax.shard_map(
        body,
        mesh=mesh,
        in_specs=(
            P(None, "gx", "gy", None),
            P("gx", "gy", None),
            P("gx", "gy", None),
            P("gx", "gy", None),
            P("gx", "gy", None),
            P("gx", "gy"),
        ),
        out_specs=(P(None, "gx", "gy", None), P("gx", "gy", None)),
        check_vma=False,
    )
```

time: 140 us -> 65.1 us (0.46)
  Pallas kernels: 0 us -> 61.4 us
  starting transfers between devices: 58.8 us -> 0 us
  matrix products: 30.4 us -> 0 us
  waiting for transfers between devices: 24.6 us -> 0 us
  other arithmetic: 13.9 us -> 0 us
  local copies, waits for them, and re-layouts: 10.2 us -> 2.16 us
    pallas_call x0 -> x1, Pallas kernels: none -> 61.4 us  [body(): pl.pallas_call(kernel, out_shape=(jax.ShapeDtypeStruct((3, 8, 8, 128), F3...]
    all_to_all x4 -> x0, starting transfers between devices: 34.3 us -> none  [the longest x1 18.2 us: body(): lax.all_to_all(ytrans, 'gx', split_axis=2, concat_axis=1, tiled=True)]
    dot_general x9 -> x0, matrix products: 30.4 us -> none  [the longest x1 6.61 us: body(): jnp.dot(onehot_depth.T, charge_flat[:, None] * onehot_flat, precision=hig...]
    ppermute x4 -> x0, starting transfers between devices: 24.4 us -> none  [the longest x2 14.9 us: with_halo(): after = lax.ppermute(initial, axis, down)]
    all_to_all x4 -> x0, waiting for transfers between devices: 23.4 us -> none  [the longest x1 10.1 us: body(): lax.all_to_all(xback, 'gx', split_axis=1, concat_axis=2, tiled=True)]
    reduce_sum x2 -> x0, other arithmetic: 5.74 us -> none  [the longest x1 3.68 us: pair_force(): return jnp.sum(weight[None] * delta, axis=2)]
    all_to_all x4 -> x0, other arithmetic: 3.8 us -> none  [the longest x1 0.95 us: body(): lax.all_to_all(yback, 'gy', split_axis=2, concat_axis=0, tiled=True)]
    unnamed x18 -> x4, local copies, waits for them, and re-layouts: 5.44 us -> 2.16 us
  transfers between devices with their start and end apart: 8 -> 0, of which waited for: 4 -> 0; matrix products, arithmetic and copies ran while one was open for 15% -> 0% of each run, Pallas kernels for 0% -> 0%
where the time goes in v1:
time: 65.1 us; the launch traced here: 64.9 us
  Pallas kernels  61.4 us (94%)
  local copies, waits for them, and re-layouts  2.16 us (3%)
  between operations  1.29 us (2%)
    pallas_call x1, Pallas kernels, body(): pl.pallas_call(kernel, out_shape=(jax.ShapeDtypeStruct((3, 8, 8, 128), F3...  61.4 us
    unnamed x4, local copies, waits for them, and re-layouts  2.16 us

profile of v1, /device:TPU:1, one launch (start us, length us, event | category | flops | bytes accessed | tf_op | source)
XLA Modules:
  0.0 64.9 jit_solution(1486062973236122255)
XLA Ops:
  1.3 61.4 %patch_forces_and_grid.1 = (f32[3,8,8,128]{3,2,1,0:T(8,128)}, f32[8,8,128]{2,1,0:T(8,128)}) custom-call(s32[1,1,32]{2,1,0:T(1,128)} %patch_ref.1, s32[1,1,32]{2,1,0:T(1,128)} %near_s.1, s32[1,1]{1,0:T(1,128)S(6)} %copy.14.count_s, s32[1,1,32]{2,1,0:T(1,128)} %patch_ref.1, f32[3,8,8,128]{3,2,1,0:T(8,128)} %pos_hbm.1, f32[8,8,128]{2,1,0:T(8,128)} %chg_hbm.1, ...), custom_call_target="tpu_custom_call" | custom-call | tf_op jit(solution)/shard_map/patch_forces_and_grid/pallas_call | solution.py:426
  62.7 0.0 copy-start
  62.7 1.5 %copy.15 = f32[3,8,8,128]{3,2,1,0:T(8,128)} copy(f32[3,8,8,128]{3,2,1,0:T(8,128)} %get-tuple-element.4) | data formatting | bytes 196608
  64.3 0.0 copy-done
  64.3 0.6 copy.16
Async XLA Ops:
  62.7 1.6 %copy-start = (f32[8,8,128]{2,1,0:T(8,128)S(1)}, f32[8,8,128]{2,1,0:T(8,128)}, u32[]{:S(2)}) copy-start(f32[8,8,128]{2,1,0:T(8,128)} %get-tuple-element.5) | copy-start | bytes 98308

commit v2 on v1

--- a/solution.py
+++ b/solution.py
@@ -73,10 +73,9 @@
 
 
 def kernel(
-    patch_s,
-    near_s,
-    count_s,
-    patch_ref,
+    patch_hbm,
+    near_hbm,
+    count_hbm,
     pos_hbm,
     chg_hbm,
     cell_hbm,
@@ -84,20 +83,22 @@
     casy_hbm,
     casx_hbm,
     casxt_hbm,
-    forces_hbm,
-    recip_hbm,
+    forces_ref,
+    recip_ref,
+    patch_s,
+    near_s,
+    patch_ref,
+    count_ref,
     pos_ref,
     chg_ref,
     cell_ref,
-    forces_ref,
-    recip_ref,
     casz,
     casy,
     casx,
     casxt,
     halo,
-    onehot,
     grid_t,
+    sampled,
     influence,
     second,
     task_force,
@@ -110,7 +111,6 @@
     send_d,
     recv_d,
     load_sem,
-    store_sem,
     halo_send,
     halo_recv,
     ex_send,
@@ -124,11 +124,20 @@
     left = lax.rem(gy + NY - 1, NY)
     chip_y, chip_z, core = gx // 16, (gx // 2) % 8, gx % 2
 
-    def column_peer(k):
-        dc, dz, dy = k % 2, (k // 2) % 8, k // 16
-        return (
-            lax.rem(chip_y + dy, 8) * 16 + lax.rem(chip_z + dz, 8) * 2 + lax.rem(core + dc, 2)
-        )
+    across = [
+        lax.rem(chip_z + dz, 8) * 2 + lax.rem(core + dc, 2) for dz in range(8) for dc in range(2)
+    ]
+
+    def each_column_peer(visit):
+        def chip_row(i, carry):
+            base = lax.rem(chip_y + 12 - i - i // 4, 8) * 16
+            for other in across:
+                visit(base + other)
+            return carry
+
+        lax.fori_loop(0, 7, chip_row, 0)
+        for other in across[1:]:
+            visit(chip_y * 16 + other)
 
     loads = [
         pltpu.make_async_copy(src, dst, load_sem.at[i])
@@ -136,17 +145,22 @@
             (
                 (cell_hbm, cell_ref),
                 (chg_hbm, chg_ref),
-                (pos_hbm, pos_ref),
                 (casz_hbm, casz),
                 (casy_hbm, casy),
                 (casx_hbm, casx),
                 (casxt_hbm, casxt),
+                (pos_hbm, pos_ref),
+                (patch_hbm, patch_s),
+                (near_hbm, near_s),
+                (patch_hbm, patch_ref),
+                (count_hbm, count_ref),
             )
         )
     ]
-    for load in loads:
+    for load in loads[:2]:
         load.start()
-    tables = loads[3:]
+    tables = loads[2:6]
+    task_loads = loads[7:]
 
     barrier = pltpu.get_barrier_semaphore()
     for d in range(1, NY):
@@ -157,57 +171,44 @@
         for py in (left, right):
             pl.semaphore_signal(barrier, 1, device_id={"gx": px, "gy": py}, device_id_type=MESH_ID)
 
-    def greet(k, carry):
-        pl.semaphore_signal(
-            barrier, 1, device_id={"gx": column_peer(k), "gy": gy}, device_id_type=MESH_ID
+    each_column_peer(
+        lambda peer: pl.semaphore_signal(
+            barrier, 1, device_id={"gx": peer, "gy": gy}, device_id_type=MESH_ID
         )
-        return carry
-
-    lax.fori_loop(1, NX, greet, 0)
-
-    for load in loads[:3]:
-        load.wait()
-
-    for r in range(8):
-        for c in range(3):
-            halo[r + 1, 1:9, c, :] = pos_ref[c, r]
-        halo[r + 1, 1:9, 3, :] = chg_ref[r]
-
-    z_row = lax.broadcasted_iota(jnp.int32, (GZ, 256), 0)
+    )
+
+    for load in loads[2:]:
+        load.start()
+    loads[0].wait()
+    loads[1].wait()
+
     eight = lax.broadcasted_iota(jnp.int32, (8, 256), 0)
+    z_lane = lax.broadcasted_iota(jnp.int32, (128, GZ), 1)
+
+    def atoms_of(ref, x, s):
+        return jnp.concatenate([ref[2 * x, s : s + 1, :], ref[2 * x + 1, s : s + 1, :]], axis=1)
 
     def deposit(x, carry):
+        planes = jnp.concatenate([cell_ref[2 * x], cell_ref[2 * x + 1]], axis=0) // 128
+        planes = jnp.transpose(planes)
         for s in range(8):
-            cells = jnp.concatenate(
-                [cell_ref[2 * x, s : s + 1, :], cell_ref[2 * x + 1, s : s + 1, :]], axis=1
+            cells = atoms_of(cell_ref, x, s)
+            charge = atoms_of(chg_ref, x, s)
+            hot = jnp.concatenate(
+                [
+                    jnp.where(z_lane == planes[:, 8 * r + s : 8 * r + s + 1], 1.0, 0.0).astype(BF16)
+                    for r in range(2)
+                ],
+                axis=0,
             )
-            charge = jnp.concatenate(
-                [chg_ref[2 * x, s : s + 1, :], chg_ref[2 * x + 1, s : s + 1, :]], axis=1
-            )
-            hot = jnp.where(z_row == cells // 128, 1.0, 0.0).astype(BF16)
-            onehot[x * 8 + s] = hot
             high = charge.astype(BF16).astype(F32)
             rows = jnp.where(eight < 4, high, charge - high)
             rows = jnp.where(eight % 4 == cells % 4, rows, 0.0).astype(BF16)
-            part = mxu(rows, hot, ((1,), (1,)))
+            part = mxu(rows, hot)
             grid_t[x, s] = part[0:4] + part[4:8]
         return carry
 
-    lax.fori_loop(0, 4, deposit, 0)
-
-    kx = lax.broadcasted_iota(jnp.int32, (GX, 128), 0)
-    lane = lax.broadcasted_iota(jnp.int32, (GX, 128), 1)
-    kz = gy * 32 + lane % 32
-    ky = gx * 2 + (lane // 32) % 2
-
-    def wave(freq, length):
-        part = jnp.minimum(freq, length - freq).astype(F32) * (1.0 / length)
-        return part * part
-
-    wave_sq = wave(kz, GZ) + wave(kx, GX) + wave(ky, GY)
-    influence[...] = jnp.where(
-        wave_sq > 0, 1.0 / (64.0 * jnp.where(wave_sq > 0, wave_sq, 1.0)), 0.0
-    )
+    lax.fori_loop(0, 4, deposit, 0, unroll=True)
 
     tables[0].wait()
     ztrans = right_table(grid_t[...].reshape(128, GZ), casz)
@@ -243,9 +244,8 @@
         ).wait()
 
     def column_exchange(src, dst, which):
-        def send(i, carry):
-            peer = column_peer(NX - 1 - i)
-            pltpu.make_async_remote_copy(
+        each_column_peer(
+            lambda peer: pltpu.make_async_remote_copy(
                 src.at[peer],
                 dst.at[gx],
                 ex_send.at[which],
@@ -253,9 +253,7 @@
                 device_id={"gx": peer, "gy": gy},
                 device_id_type=MESH_ID,
             ).start()
-            return carry
-
-        lax.fori_loop(0, NX - 1, send, 0)
+        )
         dst[gx] = src[gx]
 
     def column_wait(src, dst, which):
@@ -269,6 +267,32 @@
         ).wait()
 
     row_exchange(send_a, recv_a, 0)
+
+    kx = lax.broadcasted_iota(jnp.int32, (GX, 128), 0)
+    lane = lax.broadcasted_iota(jnp.int32, (GX, 128), 1)
+    kz = gy * 32 + lane % 32
+    ky = gx * 2 + (lane // 32) % 2
+
+    def wave(freq, length):
+        part = jnp.minimum(freq, length - freq).astype(F32) * (1.0 / length)
+        return part * part
+
+    wave_sq = wave(kz, GZ) + wave(kx, GX) + wave(ky, GY)
+    influence[...] = jnp.where(
+        wave_sq > 0, 1.0 / (64.0 * jnp.where(wave_sq > 0, wave_sq, 1.0)), 0.0
+    )
+
+    tables[1].wait()
+    row_wait(send_a, recv_a, 0)
+    ytrans = left_table(casy, recv_a[...].reshape(GY, 128))
+    send_b[...] = ytrans.reshape(NX, 2, 128)
+    column_exchange(send_b, recv_b, 1)
+
+    loads[6].wait()
+    for r in range(8):
+        for c in range(3):
+            halo[r + 1, 1:9, c, :] = pos_ref[c, r]
+        halo[r + 1, 1:9, 3, :] = chg_ref[r]
 
     halo_copies = []
     for n, (dx, dy) in enumerate(
@@ -291,13 +315,33 @@
         copy.start()
         halo_copies.append(copy)
 
-    tables[1].wait()
-    row_wait(send_a, recv_a, 0)
-    ytrans = left_table(casy, recv_a[...].reshape(GY, 128))
-    send_b[...] = ytrans.reshape(NX, 2, 128)
-    column_exchange(send_b, recv_b, 1)
-
-    for copy in halo_copies:
+    tables[2].wait()
+    tables[3].wait()
+    column_wait(send_b, recv_b, 1)
+    lanes = lane_block((NX, 128))
+    low_half = lax.broadcasted_iota(jnp.int32, (NX, 128), 1) < 64
+    lines = [recv_b[:, e, :] for e in range(2)]
+    turned = [[turn(lines[e], d) for d in range(4)] for e in range(2)]
+    packed = []
+    for x in range(4):
+        value = pick([turned[b % 2][(b - x) % 4] for b in range(4)], lanes)
+        high = value.astype(BF16).astype(F32)
+        packed.append(jnp.where(low_half, high, value - high).astype(BF16))
+    packed = jnp.concatenate(packed, axis=0)
+    total = mxu(casx[0], packed) + mxu(casx[1], packed)
+    scaled = (total + pltpu.roll(total, 64, 1)) * influence[...]
+    high = scaled.astype(BF16).astype(F32)
+    half = lax.broadcasted_iota(jnp.int32, (GX, 128), 1) < 64
+    packed = jnp.where(half, high, scaled - high).astype(BF16)
+    total = mxu(casxt[0], packed) + mxu(casxt[1], packed)
+    xback = total + pltpu.roll(total, 64, 1)
+    plain = [xback[128 * x : 128 * x + 128] for x in range(4)]
+    moved = [turn(p, 1) for p in plain]
+    send_c[:, 0, :] = pick([plain[0], moved[1], plain[2], moved[3]], lanes)
+    send_c[:, 1, :] = pick([moved[0], plain[1], moved[2], plain[3]], lanes)
+    column_exchange(send_c, recv_c, 2)
+
+    for copy in task_loads + halo_copies:
         copy.wait()
 
     def task_group(g, carry):
@@ -338,7 +382,7 @@
     lax.fori_loop(0, TASKS // 8, task_group, 0)
     slot = lax.broadcasted_iota(jnp.int32, (64, TASKS), 1)
     owner = lax.broadcasted_iota(jnp.int32, (64, TASKS), 0)
-    acts = jnp.where((owner == patch_ref[0]) & (slot < count_s[0, 0]), 1.0, 0.0).astype(BF16)
+    acts = jnp.where((owner == patch_ref[0]) & (slot < count_ref[...]), 1.0, 0.0).astype(BF16)
     for c in range(3):
         force = task_force[c]
         high = force.astype(BF16)
@@ -347,34 +391,6 @@
         low = (rest - mid.astype(F32)).astype(BF16)
         total = mxu(acts, high) + (mxu(acts, mid) + mxu(acts, low))
         forces_ref[c] = total.reshape(8, 8, 128)
-    forces_out = pltpu.make_async_copy(forces_ref, forces_hbm, store_sem.at[0])
-    forces_out.start()
-
-    tables[2].wait()
-    tables[3].wait()
-    column_wait(send_b, recv_b, 1)
-    lanes = lane_block((NX, 128))
-    low_half = lax.broadcasted_iota(jnp.int32, (NX, 128), 1) < 64
-    lines = [recv_b[:, e, :] for e in range(2)]
-    turned = [[turn(lines[e], d) for d in range(4)] for e in range(2)]
-    packed = []
-    for x in range(4):
-        value = pick([turned[b % 2][(b - x) % 4] for b in range(4)], lanes)
-        high = value.astype(BF16).astype(F32)
-        packed.append(jnp.where(low_half, high, value - high).astype(BF16))
-    packed = jnp.concatenate(packed, axis=0)
-    total = mxu(casx[0], packed) + mxu(casx[1], packed)
-    scaled = (total + pltpu.roll(total, 64, 1)) * influence[...]
-    high = scaled.astype(BF16).astype(F32)
-    half = lax.broadcasted_iota(jnp.int32, (GX, 128), 1) < 64
-    packed = jnp.where(half, high, scaled - high).astype(BF16)
-    total = mxu(casxt[0], packed) + mxu(casxt[1], packed)
-    xback = total + pltpu.roll(total, 64, 1)
-    plain = [xback[128 * x : 128 * x + 128] for x in range(4)]
-    moved = [turn(p, 1) for p in plain]
-    send_c[:, 0, :] = pick([plain[0], moved[1], plain[2], moved[3]], lanes)
-    send_c[:, 1, :] = pick([moved[0], plain[1], moved[2], plain[3]], lanes)
-    column_exchange(send_c, recv_c, 2)
 
     column_wait(send_c, recv_c, 2)
     yback = left_table(casy, recv_c[...].reshape(GY, 128))
@@ -391,27 +407,24 @@
             )
         rows.append(jnp.concatenate(halves, axis=1))
     field = right_table(jnp.concatenate(rows, axis=0), casz) * (1.0 / (GX * GY * GZ))
-    grid_t[...] = field.reshape(4, 8, 4, GZ)
-
-    def sample(x, carry):
+    for h in range(2):
+        half_z = field[:, 128 * h : 128 * h + 128].reshape(32, 4, 128)
+        sampled[:, 4 * h : 4 * h + 4, :] = half_z
+
+    row_code = lax.broadcasted_iota(jnp.int32, (8, 128), 0)
+    for r in range(8):
         for s in range(8):
-            cells = jnp.concatenate(
-                [cell_ref[2 * x, s : s + 1, :], cell_ref[2 * x + 1, s : s + 1, :]], axis=1
+            cells = jnp.broadcast_to(cell_ref[r, s : s + 1, :], (8, 128))
+            planes = cells // 128
+            got = jnp.take_along_axis(sampled[(r // 2) * 8 + s], planes % 128, axis=1)
+            code = (planes // 128) * 4 + cells % 4
+            recip_ref[r, s : s + 1, :] = jnp.sum(
+                jnp.where(row_code == code, got, 0.0), axis=0, keepdims=True
             )
-            value = grid_t[x, s]
-            high = value.astype(BF16).astype(F32)
-            both = jnp.concatenate([high, value - high], axis=0).astype(BF16)
-            got = mxu(both, onehot[x * 8 + s])
-            got = jnp.sum(jnp.where(eight % 4 == cells % 4, got, 0.0), axis=0, keepdims=True)
-            recip_ref[2 * x, s : s + 1, :] = got[:, :128]
-            recip_ref[2 * x + 1, s : s + 1, :] = got[:, 128:]
-        return carry
-
-    lax.fori_loop(0, 4, sample, 0)
-    recip_out = pltpu.make_async_copy(recip_ref, recip_hbm, store_sem.at[1])
-    recip_out.start()
-    forces_out.wait()
-    recip_out.wait()
+
+
+def in_hbm(array):
+    return pltpu.with_memory_space_constraint(array, pltpu.HBM)
 
 
 def body(positions, charges, cell_index, task_patch, task_near, task_count):
@@ -420,30 +433,30 @@
     order = (4 * np.arange(NX)[None, :] + np.arange(4)[:, None]).reshape(-1)
     casx = cas_split(GX, order)
     casxt = np.ascontiguousarray(np.swapaxes(casx, 1, 2))
-    vmem = pl.BlockSpec(memory_space=pltpu.VMEM)
-    smem = pl.BlockSpec(memory_space=pltpu.SMEM)
     hbm = pl.BlockSpec(memory_space=pltpu.HBM)
     return pl.pallas_call(
         kernel,
         out_shape=(
-            jax.ShapeDtypeStruct((3, 8, 8, 128), F32),
-            jax.ShapeDtypeStruct((8, 8, 128), F32),
+            pltpu.VMEM((3, 8, 8, 128), F32),
+            pltpu.VMEM((8, 8, 128), F32),
         ),
-        in_specs=[smem] * 3 + [vmem] + [hbm] * 7,
-        out_specs=(hbm, hbm),
+        in_specs=[hbm] * 10,
+        out_specs=(pl.BlockSpec(memory_space=pltpu.VMEM),) * 2,
         scratch_shapes=[
+            pltpu.SMEM((1, 1, TASKS), jnp.int32),
+            pltpu.SMEM((1, 1, TASKS), jnp.int32),
+            pltpu.VMEM((1, 1, TASKS), jnp.int32),
+            pltpu.VMEM((1, 1), jnp.int32),
             pltpu.VMEM((3, 8, 8, 128), F32),
             pltpu.VMEM((8, 8, 128), F32),
             pltpu.VMEM((8, 8, 128), jnp.int32),
-            pltpu.VMEM((3, 8, 8, 128), F32),
-            pltpu.VMEM((8, 8, 128), F32),
             pltpu.VMEM((2, GZ, GZ), BF16),
             pltpu.VMEM((2, GY, GY), BF16),
             pltpu.VMEM((2, GX, GX), BF16),
             pltpu.VMEM((2, GX, GX), BF16),
             pltpu.VMEM((10, 10, 4, 128), F32),
-            pltpu.VMEM((32, GZ, 256), BF16),
             pltpu.VMEM((4, 8, 4, GZ), F32),
+            pltpu.VMEM((32, 8, 128), F32),
             pltpu.VMEM((GX, 128), F32),
             pltpu.VMEM((32, 128), F32),
             pltpu.VMEM((3, TASKS, 128), F32),
@@ -455,29 +468,27 @@
             pltpu.VMEM((NX, 2, 128), F32),
             pltpu.VMEM((NY, 32, 128), F32),
             pltpu.VMEM((NY, 32, 128), F32),
-            pltpu.SemaphoreType.DMA((7,)),
-            pltpu.SemaphoreType.DMA((2,)),
+            pltpu.SemaphoreType.DMA((11,)),
             pltpu.SemaphoreType.DMA((8,)),
             pltpu.SemaphoreType.DMA((8,)),
             pltpu.SemaphoreType.DMA((4,)),
             pltpu.SemaphoreType.DMA((4,)),
         ],
         compiler_params=pltpu.CompilerParams(
-            collective_id=0, has_side_effects=True, vmem_limit_bytes=67_043_328
+            collective_id=0, has_side_effects=True, vmem_limit_bytes=60 * 1024 * 1024
         ),
         name="patch_forces_and_grid",
     )(
-        task_patch,
-        task_near,
+        in_hbm(task_patch),
+        in_hbm(task_near),
         task_count,
-        task_patch,
-        positions,
-        charges,
-        cell_index,
-        casz,
-        casy,
-        casx,
-        casxt,
+        in_hbm(positions),
+        in_hbm(charges),
+        in_hbm(cell_index),
+        in_hbm(jnp.asarray(casz)),
+        in_hbm(jnp.asarray(casy)),
+        in_hbm(jnp.asarray(casx)),
+        in_hbm(jnp.asarray(casxt)),
     )
 
 

time: 65.1 us -> 58.2 us (0.89)
  Pallas kernels: 61.4 us -> 55.5 us
  local copies, waits for them, and re-layouts: 2.16 us -> 1.26 us
    pallas_call x1, Pallas kernels: 61.4 us -> 55.5 us  [body(): pl.pallas_call(kernel, out_shape=(pltpu.VMEM((3, 8, 8, 128), F32), pltpu....]
    unnamed x4 -> x2, local copies, waits for them, and re-layouts: 2.16 us -> 1.26 us
where the time goes in v2:
time: 58.2 us; the launch traced here: 58 us
  Pallas kernels  55.5 us (95%)
  between operations  1.29 us (2%)
  local copies, waits for them, and re-layouts  1.26 us (2%)
    pallas_call x1, Pallas kernels, body(): pl.pallas_call(kernel, out_shape=(pltpu.VMEM((3, 8, 8, 128), F32), pltpu....  55.5 us
    unnamed x2, local copies, waits for them, and re-layouts  1.26 us

profile of v2, /device:TPU:1, one launch (start us, length us, event | category | flops | bytes accessed | tf_op | source)
XLA Modules:
  0.0 58.0 jit_solution(3886951357034509700)
XLA Ops:
  1.3 55.5 %patch_forces_and_grid.1 = (f32[3,8,8,128]{3,2,1,0:T(8,128)S(1)}, f32[8,8,128]{2,1,0:T(8,128)S(1)}) custom-call(s32[1,1,32]{2,1,0:T(1,128)} %patch_hbm.1, s32[1,1,32]{2,1,0:T(1,128)} %near_hbm.1, s32[1,1]{1,0:T(1,128)S(6)} %copy.16.count_hbm, f32[3,8,8,128]{3,2,1,0:T(8,128)} %pos_hbm.1, f32[8,8,128]{2,1,0:T(8,128)} %chg_hbm.1, s32[8,8,128]{2,1,0:T(8,128)} %cell_hbm.1, ...), custom_call_target="tpu_custom_call" | custom-call | tf_op jit(solution)/shard_map/patch_forces_and_grid/pallas_call | solution.py:437
  56.8 0.6 %copy.14 = f32[3,8,8,128]{3,2,1,0:T(8,128)} copy(f32[3,8,8,128]{3,2,1,0:T(8,128)S(1)} %get-tuple-element.2) | data formatting | bytes 196608
  57.4 0.6 %copy.15 = f32[8,8,128]{2,1,0:T(8,128)} copy(f32[8,8,128]{2,1,0:T(8,128)S(1)} %get-tuple-element.3) | data formatting | bytes 65536

commit v3 on v2

--- a/solution.py
+++ b/solution.py
@@ -54,6 +54,15 @@
     m = value.shape[0]
     both = mxu(jnp.concatenate([high, low], axis=0), table[0])
     return both[:m] + both[m:] + mxu(high, table[1])
+
+
+def x_transform(table, packed):
+    halves = []
+    for h in range(2):
+        rows = slice(GX // 2 * h, GX // 2 * (h + 1))
+        halves.append(mxu(table[0, rows], packed) + mxu(table[1, rows], packed))
+    total = jnp.concatenate(halves, axis=0)
+    return total + pltpu.roll(total, 64, 1)
 
 
 def lane_block(shape):
@@ -115,6 +124,7 @@
     halo_recv,
     ex_send,
     ex_recv,
+    line_sem,
 ):
     gx = lax.axis_index("gx")
     gy = lax.axis_index("gy")
@@ -124,19 +134,21 @@
     left = lax.rem(gy + NY - 1, NY)
     chip_y, chip_z, core = gx // 16, (gx // 2) % 8, gx % 2
 
+    far_first = (4, 3, 5, 2, 6, 1, 7, 0)
     across = [
-        lax.rem(chip_z + dz, 8) * 2 + lax.rem(core + dc, 2) for dz in range(8) for dc in range(2)
+        lax.rem(chip_z + dz, 8) * 2 + lax.rem(core + dc, 2) for dz in far_first for dc in (1, 0)
     ]
 
     def each_column_peer(visit):
         def chip_row(i, carry):
-            base = lax.rem(chip_y + 12 - i - i // 4, 8) * 16
+            dy = 4 + (1 - 2 * (i % 2)) * ((i + 1) // 2)
+            base = lax.rem(chip_y + dy, 8) * 16
             for other in across:
                 visit(base + other)
             return carry
 
         lax.fori_loop(0, 7, chip_row, 0)
-        for other in across[1:]:
+        for other in across[:-1]:
             visit(chip_y * 16 + other)
 
     loads = [
@@ -163,19 +175,22 @@
     task_loads = loads[7:]
 
     barrier = pltpu.get_barrier_semaphore()
-    for d in range(1, NY):
-        pl.semaphore_signal(
-            barrier, 1, device_id={"gx": gx, "gy": lax.rem(gy + d, NY)}, device_id_type=MESH_ID
-        )
+
+    def signal(semaphore, px, py):
+        pl.semaphore_signal(semaphore, 1, device_id={"gx": px, "gy": py}, device_id_type=MESH_ID)
+
+    ring_y = [
+        lax.rem(chip_y + dy, 8) * 16 + chip_z * 2 + core for dy in far_first[:-1]
+    ]
+    for d in far_first[:-1]:
+        signal(barrier, gx, lax.rem(gy + d, NY))
+    for peer in ring_y:
+        signal(barrier, peer, gy)
+    for other in across[:-1]:
+        signal(barrier, chip_y * 16 + other, gy)
     for px in (up, down):
         for py in (left, right):
-            pl.semaphore_signal(barrier, 1, device_id={"gx": px, "gy": py}, device_id_type=MESH_ID)
-
-    each_column_peer(
-        lambda peer: pl.semaphore_signal(
-            barrier, 1, device_id={"gx": peer, "gy": gy}, device_id_type=MESH_ID
-        )
-    )
+            signal(barrier, px, py)
 
     for load in loads[2:]:
         load.start()
@@ -218,7 +233,7 @@
         for m in range(4):
             send_a[4 * h + m] = pick([turn(parts[x], x - m) for x in range(4)], quarter)
 
-    pl.semaphore_wait(barrier, NY - 1 + 4 + NX - 1)
+    pl.semaphore_wait(barrier, 7 + 7 + 15 + 4)
 
     def row_exchange(src, dst, which):
         for d in (4, 3, 5, 2, 6, 1, 7):
@@ -267,6 +282,8 @@
         ).wait()
 
     row_exchange(send_a, recv_a, 0)
+    for peer in ring_y:
+        signal(line_sem, peer, gy)
 
     kx = lax.broadcasted_iota(jnp.int32, (GX, 128), 0)
     lane = lax.broadcasted_iota(jnp.int32, (GX, 128), 1)
@@ -286,6 +303,7 @@
     row_wait(send_a, recv_a, 0)
     ytrans = left_table(casy, recv_a[...].reshape(GY, 128))
     send_b[...] = ytrans.reshape(NX, 2, 128)
+    pl.semaphore_wait(line_sem, 7)
     column_exchange(send_b, recv_b, 1)
 
     loads[6].wait()
@@ -328,13 +346,11 @@
         high = value.astype(BF16).astype(F32)
         packed.append(jnp.where(low_half, high, value - high).astype(BF16))
     packed = jnp.concatenate(packed, axis=0)
-    total = mxu(casx[0], packed) + mxu(casx[1], packed)
-    scaled = (total + pltpu.roll(total, 64, 1)) * influence[...]
+    scaled = x_transform(casx, packed) * influence[...]
     high = scaled.astype(BF16).astype(F32)
     half = lax.broadcasted_iota(jnp.int32, (GX, 128), 1) < 64
     packed = jnp.where(half, high, scaled - high).astype(BF16)
-    total = mxu(casxt[0], packed) + mxu(casxt[1], packed)
-    xback = total + pltpu.roll(total, 64, 1)
+    xback = x_transform(casxt, packed)
     plain = [xback[128 * x : 128 * x + 128] for x in range(4)]
     moved = [turn(p, 1) for p in plain]
     send_c[:, 0, :] = pick([plain[0], moved[1], plain[2], moved[3]], lanes)
@@ -473,6 +489,7 @@
             pltpu.SemaphoreType.DMA((8,)),
             pltpu.SemaphoreType.DMA((4,)),
             pltpu.SemaphoreType.DMA((4,)),
+            pltpu.SemaphoreType.REGULAR,
         ],
         compiler_params=pltpu.CompilerParams(
             collective_id=0, has_side_effects=True, vmem_limit_bytes=60 * 1024 * 1024

time: 58.2 us -> 53.1 us (0.912)
  Pallas kernels: 55.5 us -> 50.3 us
    pallas_call x1, Pallas kernels: 55.5 us -> 50.3 us  [body(): pl.pallas_call(kernel, out_shape=(pltpu.VMEM((3, 8, 8, 128), F32), pltpu....]
where the time goes in v3:
time: 53.1 us; the launch traced here: 52.9 us
  Pallas kernels  50.3 us (95%)
  between operations  1.29 us (2%)
  local copies, waits for them, and re-layouts  1.26 us (2%)
    pallas_call x1, Pallas kernels, body(): pl.pallas_call(kernel, out_shape=(pltpu.VMEM((3, 8, 8, 128), F32), pltpu....  50.3 us
    unnamed x2, local copies, waits for them, and re-layouts  1.26 us

profile of v3, /device:TPU:1, one launch (start us, length us, event | category | flops | bytes accessed | tf_op | source)
XLA Modules:
  0.0 52.9 jit_solution(7422801344354230937)
XLA Ops:
  1.3 50.3 %patch_forces_and_grid.1 = (f32[3,8,8,128]{3,2,1,0:T(8,128)S(1)}, f32[8,8,128]{2,1,0:T(8,128)S(1)}) custom-call(s32[1,1,32]{2,1,0:T(1,128)} %patch_hbm.1, s32[1,1,32]{2,1,0:T(1,128)} %near_hbm.1, s32[1,1]{1,0:T(1,128)S(6)} %copy.16.count_hbm, f32[3,8,8,128]{3,2,1,0:T(8,128)} %pos_hbm.1, f32[8,8,128]{2,1,0:T(8,128)} %chg_hbm.1, s32[8,8,128]{2,1,0:T(8,128)} %cell_hbm.1, ...), custom_call_target="tpu_custom_call" | custom-call | tf_op jit(solution)/shard_map/patch_forces_and_grid/pallas_call | solution.py:453
  51.6 0.6 %copy.14 = f32[3,8,8,128]{3,2,1,0:T(8,128)} copy(f32[3,8,8,128]{3,2,1,0:T(8,128)S(1)} %get-tuple-element.2) | data formatting | bytes 196608
  52.3 0.6 %copy.15 = f32[8,8,128]{2,1,0:T(8,128)} copy(f32[8,8,128]{2,1,0:T(8,128)S(1)} %get-tuple-element.3) | data formatting | bytes 65536
